TPU v7x, 32 devices: a whole 2x2x4 slice. The times are simulated.
32 devices in a mesh: seq: 8 (over z, y), grp: 4 (over x, core).
Axes of the slice: x: 2, y: 2, z: 4, core: 2. Of those that a mesh axis runs over, the one named last changes fastest.
Arguments:
- queries: bfloat16 [8192, 1024], P(('seq', 'grp')), may hold values from -5 to 5
- key_rows: bfloat16 [8192, 128], P(('seq', 'grp')), may hold values from -5 to 5
- value_rows: bfloat16 [8192, 128], P(('seq', 'grp')), may hold values from -6 to 6
- out_grad: bfloat16 [8192, 1024], P(('seq', 'grp')), may hold values from -6 to 6
- segment: int32 [8192], P(('seq', 'grp')), may hold values from 0 to 9, never falling along the last dimension, each value on 1 to 1536 neighbouring positions
Outputs:
- attended: bfloat16 [8192, 1024], P(('seq', 'grp'))
- query_grad: bfloat16 [8192, 1024], P(('seq', 'grp'))
- key_grad: float32 [8192, 128], P(('seq', 'grp'))
- value_grad: float32 [8192, 128], P(('seq', 'grp'))
Inputs may be any that keep to these rules, and one draw needn't show every extreme that they name: `segment`: segment numbers start at 0 and never fall along the sequence; every document holds 1 to 1536 tokens, and one holds exactly 1536.
All inputs are finite; a program needn't handle non-finite values.
Results may differ from a plain program's by a relative error of at most 0.019.
Values may be sent and summed in bfloat16 or wider, within the bound.
A program may use at most 64 MiB of HBM per device.

v0:
```python
import jax
import jax.numpy as jnp
from jax import lax
from jax.sharding import PartitionSpec as P

SPAN = 6


def shifted(value, axis, steps):
    count = lax.axis_size(axis)
    first, last = (max(0, -steps), min(count, count - steps))
    return lax.ppermute(value, axis, [(source, source + steps) for source in range(first, last)])


def on_device(queries, key_rows, value_rows, out_grad, segment):
    tokens = queries.shape[0]
    head_width = key_rows.shape[1]
    head_count = queries.shape[1] // head_width
    score_scale = head_width ** (-0.5)
    groups = lax.axis_size("grp")
    own_start = (lax.axis_index("seq") * groups + lax.axis_index("grp")) * tokens
    query_pos = own_start + jnp.arange(tokens, dtype=jnp.int32)
    query_heads = queries.reshape(tokens, head_count, head_width)
    grad_heads = out_grad.reshape(tokens, head_count, head_width)
    entries = [(key_rows, value_rows, segment, own_start)]
    for distance in range(1, SPAN + 1):
        arrived = shifted((key_rows, value_rows, segment), ("seq", "grp"), distance)
        entries.append((arrived[0], arrived[1], arrived[2], own_start - distance * tokens))

    def visible_of(entry_seg, entry_start):
        key_pos = entry_start + jnp.arange(entry_seg.shape[0], dtype=jnp.int32)
        allowed = (
            (entry_seg[None, :] == segment[:, None])
            & (key_pos[None, :] <= query_pos[:, None])
            & (key_pos[None, :] >= 0)
        )
        return allowed[:, None, :]

    def scores_of(entry_keys):
        return (
            jnp.einsum("thd,kd->thk", query_heads, entry_keys, preferred_element_type=jnp.float32)
            * score_scale
        )

    masks = [visible_of(entry[2], entry[3]) for entry in entries]
    running = (
        jnp.full((tokens, head_count), -1e30, jnp.float32),
        jnp.zeros((tokens, head_count), jnp.float32),
    )
    for entry, visible in zip(entries, masks):

        def first_pass(state_pair, entry=entry, visible=visible):
            row_max, row_sum = state_pair
            scores = scores_of(entry[0])
            new_max = jnp.maximum(row_max, jnp.max(jnp.where(visible, scores, -1e30), axis=-1))
            added = jnp.sum(jnp.where(visible, jnp.exp(scores - new_max[..., None]), 0.0), axis=-1)
            return (new_max, row_sum * jnp.exp(row_max - new_max) + added)

        running = first_pass(running)
    log_total = running[0] + jnp.log(running[1])
    output_sum = jnp.zeros((tokens, head_count, head_width), jnp.float32)
    for entry, visible in zip(entries, masks):

        def second_pass(partial_value, entry=entry, visible=visible):
            prob = jnp.where(visible, jnp.exp(scores_of(entry[0]) - log_total[..., None]), 0.0)
            weight = prob.astype(jnp.bfloat16)
            return partial_value + jnp.einsum(
                "thk,kd->thd", weight, entry[1], preferred_element_type=jnp.float32
            )

        output_sum = second_pass(output_sum)
    attended = output_sum.astype(jnp.bfloat16)
    row_dot = jnp.sum(grad_heads.astype(jnp.float32) * attended.astype(jnp.float32), axis=-1)
    query_total = jnp.zeros((tokens, head_count, head_width), jnp.float32)
    key_parts = []
    value_parts = []
    for entry, visible in zip(entries, masks):
        empty_rows = jnp.zeros((entry[0].shape[0], head_width), jnp.float32)

        def third_pass(triple, entry=entry, visible=visible):
            prob = jnp.where(visible, jnp.exp(scores_of(entry[0]) - log_total[..., None]), 0.0)
            weight = prob.astype(jnp.bfloat16)
            dprob = jnp.einsum(
                "thd,kd->thk", grad_heads, entry[1], preferred_element_type=jnp.float32
            )
            dscore = (score_scale * prob * (dprob - row_dot[..., None])).astype(jnp.bfloat16)
            query_next = triple[0] + jnp.einsum(
                "thk,kd->thd", dscore, entry[0], preferred_element_type=jnp.float32
            )
            key_part = jnp.einsum(
                "thk,thd->kd", dscore, query_heads, preferred_element_type=jnp.float32
            )
            value_part = jnp.einsum(
                "thk,thd->kd", weight, grad_heads, preferred_element_type=jnp.float32
            )
            return (query_next, key_part, value_part)

        query_total, key_part, value_part = third_pass((query_total, empty_rows, empty_rows))
        key_parts.append(key_part)
        value_parts.append(value_part)
    key_grad = key_parts[0]
    value_grad = value_parts[0]
    for distance in range(1, SPAN + 1):
        returned = (
            shifted(key_parts[distance].astype(jnp.bfloat16), ("seq", "grp"), -distance).astype(
                jnp.float32
            ),
            shifted(value_parts[distance].astype(jnp.bfloat16), ("seq", "grp"), -distance).astype(
                jnp.float32
            ),
        )
        key_grad = key_grad + returned[0]
        value_grad = value_grad + returned[1]
    return (
        attended.reshape(tokens, head_count * head_width),
        query_total.astype(jnp.bfloat16).reshape(tokens, head_count * head_width),
        key_grad,
        value_grad,
    )


def solution(mesh):
    in_specs = (
        P(("seq", "grp"), None),
        P(("seq", "grp"), None),
        P(("seq", "grp"), None),
        P(("seq", "grp"), None),
        P(("seq", "grp")),
    )
    out_specs = (
        P(("seq", "grp"), None),
        P(("seq", "grp"), None),
        P(("seq", "grp"), None),
        P(("seq", "grp"), None),
    )
    return jax.shard_map(
        on_device, mesh=mesh, in_specs=in_specs, out_specs=out_specs, check_vma=False
    )
```

profile of v0, /device:TPU:27, one launch (start us, length us, event | category | flops | bytes accessed | tf_op | source)
XLA Modules:
  0.0 153.1 jit_solution(542975147114110650)
XLA Ops:
  0.6 3.3 %collective-permute-start.6 = (s32[256]{0:T(256)}, s32[256]{0:T(256)S(1)}, u32[]{:S(2)}, u32[]{:S(2)}) collective-permute-start(s32[256]{0:T(256)} %param.9), channel_id=1, source_target_pairs={{0,4},{1,5},{2,6},{3,7},{4,8},{5,9},{6,10},{7,11},{8,12},{9,13},{1... | collective-permute-start | bytes 3080 | tf_op jit(solution)/shard_map/ppermute | solution.py:12
  3.9 1.9 %collective-permute-start.4 = (s32[256]{0:T(256)}, s32[256]{0:T(256)S(1)}, u32[]{:S(2)}, u32[]{:S(2)}) collective-permute-start(s32[256]{0:T(256)} %param.9), channel_id=1, source_target_pairs={{0,3},{1,4},{2,5},{3,6},{4,7},{5,8},{6,9},{7,10},{8,11},{9,12},{10... | collective-permute-start | bytes 3080 | tf_op jit(solution)/shard_map/ppermute | solution.py:12
  5.9 1.9 %collective-permute-start.2 = (s32[256]{0:T(256)}, s32[256]{0:T(256)S(1)}, u32[]{:S(2)}, u32[]{:S(2)}) collective-permute-start(s32[256]{0:T(256)} %param.9), channel_id=1, source_target_pairs={{0,2},{1,3},{2,4},{3,5},{4,6},{5,7},{6,8},{7,9},{8,10},{9,11},{10,... | collective-permute-start | bytes 3080 | tf_op jit(solution)/shard_map/ppermute | solution.py:12
  7.8 1.3 collective-permute-start.10
  9.1 1.3 collective-permute-start.8
  11.6 1.3 copy.30
  12.9 2.7 %collective-permute-start = (s32[256]{0:T(256)}, s32[256]{0:T(256)S(1)}, u32[]{:S(2)}, u32[]{:S(2)}) collective-permute-start(s32[256]{0:T(256)} %param.9), channel_id=1, source_target_pairs={{0,1},{1,2},{2,3},{3,4},{4,5},{5,6},{6,7},{7,8},{8,9},{9,10},{10,1... | collective-permute-start | bytes 3080 | tf_op jit(solution)/shard_map/ppermute | solution.py:12
  15.6 1.3 collective-permute-start.17
  16.9 1.3 collective-permute-start.16
  18.2 1.9 %collective-permute-start.15 = (bf16[256,128]{0,1:T(8,128)(2,1)S(1)}, bf16[256,128]{0,1:T(8,128)(2,1)S(1)}, u32[]{:S(2)}, u32[]{:S(2)}) collective-permute-start(bf16[256,128]{0,1:T(8,128)(2,1)S(1)} %copy.18), channel_id=1, source_target_pairs={{0,4},{1,5},{2,6},{3,7},{4,8},{5,9},{6,10},{7,11},{8,12},{9,13},{1... | collective-permute-start | bytes 196616 | tf_op jit(solution)/shard_map/ppermute | solution.py:12
  20.2 1.9 %collective-permute-start.14 = (bf16[256,128]{0,1:T(8,128)(2,1)S(1)}, bf16[256,128]{0,1:T(8,128)(2,1)S(1)}, u32[]{:S(2)}, u32[]{:S(2)}) collective-permute-start(bf16[256,128]{0,1:T(8,128)(2,1)S(1)} %copy.18), channel_id=1, source_target_pairs={{0,3},{1,4},{2,5},{3,6},{4,7},{5,8},{6,9},{7,10},{8,11},{9,12},{10... | collective-permute-start | bytes 196616 | tf_op jit(solution)/shard_map/ppermute | solution.py:12
  22.1 1.7 %and_and_fusion.6 = (pred[256,256]{0,1:T(8,128)(4,1)S(1)}, pred[256,256]{0,1:T(8,128)(4,1)S(1)}, pred[256,256]{0,1:T(8,128)(4,1)S(1)}, pred[256,256]{0,1:T(8,128...) fusion(s32[256]{0:T(256)S(1)} %iota_add_fusion.6, s32[256]{0:T(256)} %param.9, ...), kind=kLoop, calls=%fused_computation.103 | loop fusion | flops 1572864 | bytes 407040 | tf_op jit(solution)/shard_map/and | solution.py:33
  23.9 1.3 select_reduce_fusion.13
  25.2 1.9 %collective-permute-start.5 = (bf16[256,128]{1,0:T(8,128)(2,1)S(1)}, bf16[256,128]{1,0:T(8,128)(2,1)S(1)}, u32[]{:S(2)}, u32[]{:S(2)}) collective-permute-start(bf16[256,128]{1,0:T(8,128)(2,1)S(1)} %copy-done.2), channel_id=1, source_target_pairs={{0,3},{1,4},{2,5},{3,6},{4,7},{5,8},{6,9},{7,10},{8,11},{9,12},{10... | collective-permute-start | bytes 196616 | tf_op jit(solution)/shard_map/ppermute | solution.py:12
  27.3 6.0 %collective-permute-done.5 = bf16[256,128]{1,0:T(8,128)(2,1)S(1)} collective-permute-done((bf16[256,128]{1,0:T(8,128)(2,1)S(1)}, bf16[256,128]{1,0:T(8,128)(2,1)S(1)}, u32[]{:S(2)}, u32[]{:S(2)}) %collective-permute-start.5) | collective-permute-done | bytes 65568 | tf_op jit(solution)/shard_map/ppermute | solution.py:12
  33.3 1.9 %collective-permute-start.7 = (bf16[256,128]{1,0:T(8,128)(2,1)S(1)}, bf16[256,128]{1,0:T(8,128)(2,1)S(1)}, u32[]{:S(2)}, u32[]{:S(2)}) collective-permute-start(bf16[256,128]{1,0:T(8,128)(2,1)S(1)} %copy-done.2), channel_id=1, source_target_pairs={{0,4},{1,5},{2,6},{3,7},{4,8},{5,9},{6,10},{7,11},{8,12},{9,13},{1... | collective-permute-start | bytes 196616 | tf_op jit(solution)/shard_map/ppermute | solution.py:12
  35.7 5.0 %collective-permute-done.7 = bf16[256,128]{1,0:T(8,128)(2,1)S(1)} collective-permute-done((bf16[256,128]{1,0:T(8,128)(2,1)S(1)}, bf16[256,128]{1,0:T(8,128)(2,1)S(1)}, u32[]{:S(2)}, u32[]{:S(2)}) %collective-permute-start.7) | collective-permute-done | bytes 65568 | tf_op jit(solution)/shard_map/ppermute | solution.py:12
  40.7 1.3 collective-permute-start.9
  42.5 6.3 %collective-permute-done.9 = bf16[256,128]{1,0:T(8,128)(2,1)S(1)} collective-permute-done((bf16[256,128]{1,0:T(8,128)(2,1)S(1)}, bf16[256,128]{1,0:T(8,128)(2,1)S(1)}, u32[]{:S(2)}, u32[]{:S(2)}) %collective-permute-start.9) | collective-permute-done | bytes 65568 | tf_op jit(solution)/shard_map/ppermute | solution.py:12
  48.7 1.3 collective-permute-start.11
  50.5 5.4 %collective-permute-done.11 = bf16[256,128]{1,0:T(8,128)(2,1)S(1)} collective-permute-done((bf16[256,128]{1,0:T(8,128)(2,1)S(1)}, bf16[256,128]{1,0:T(8,128)(2,1)S(1)}, u32[]{:S(2)}, u32[]{:S(2)}) %collective-permute-start.11) | collective-permute-done | bytes 65568 | tf_op jit(solution)/shard_map/ppermute | solution.py:12
  56.0 3.3 %collective-permute-start.3 = (bf16[256,128]{1,0:T(8,128)(2,1)S(1)}, bf16[256,128]{1,0:T(8,128)(2,1)S(1)}, u32[]{:S(2)}, u32[]{:S(2)}) collective-permute-start(bf16[256,128]{1,0:T(8,128)(2,1)S(1)} %copy-done.2), channel_id=1, source_target_pairs={{0,2},{1,3},{2,4},{3,5},{4,6},{5,7},{6,8},{7,9},{8,10},{9,11},{10,... | collective-permute-start | bytes 196616 | tf_op jit(solution)/shard_map/ppermute | solution.py:12
  59.7 1.3 collective-permute-done.3
  61.0 6.6 %collective-permute-start.1 = (bf16[256,128]{1,0:T(8,128)(2,1)S(1)}, bf16[256,128]{1,0:T(8,128)(2,1)S(1)}, u32[]{:S(2)}, u32[]{:S(2)}) collective-permute-start(bf16[256,128]{1,0:T(8,128)(2,1)S(1)} %copy-done.2), channel_id=1, source_target_pairs={{0,1},{1,2},{2,3},{3,4},{4,5},{5,6},{6,7},{7,8},{8,9},{9,10},{10,1... | collective-permute-start | bytes 196616 | tf_op jit(solution)/shard_map/ppermute | solution.py:12
  68.9 5.2 %collective-permute-start.12 = (bf16[256,128]{0,1:T(8,128)(2,1)S(1)}, bf16[256,128]{0,1:T(8,128)(2,1)S(1)}, u32[]{:S(2)}, u32[]{:S(2)}) collective-permute-start(bf16[256,128]{0,1:T(8,128)(2,1)S(1)} %copy.18), channel_id=1, source_target_pairs={{0,1},{1,2},{2,3},{3,4},{4,5},{5,6},{6,7},{7,8},{8,9},{9,10},{10,1... | collective-permute-start | bytes 196616 | tf_op jit(solution)/shard_map/ppermute | solution.py:12
  77.8 1.1 fusion.23
  78.9 1.1 fusion.24
  80.0 1.1 fusion.25
  81.2 1.1 fusion.26
  82.9 1.1 fusion.27
  84.0 2.1 %collective-permute-start.13 = (bf16[256,128]{0,1:T(8,128)(2,1)S(1)}, bf16[256,128]{0,1:T(8,128)(2,1)S(1)}, u32[]{:S(2)}, u32[]{:S(2)}) collective-permute-start(bf16[256,128]{0,1:T(8,128)(2,1)S(1)} %copy.18), channel_id=1, source_target_pairs={{0,2},{1,3},{2,4},{3,5},{4,6},{5,7},{6,8},{7,9},{8,10},{9,11},{10,... | collective-permute-start | bytes 196616 | tf_op jit(solution)/shard_map/ppermute | solution.py:12
  87.2 8.1 %collective-permute-start.29 = (bf16[256,128]{1,0:T(8,128)(2,1)S(1)}, bf16[256,128]{1,0:T(8,128)(2,1)S(1)}, u32[]{:S(2)}, u32[]{:S(2)}) collective-permute-start(bf16[256,128]{1,0:T(8,128)(2,1)S(1)} %fusion.28), channel_id=1, source_target_pairs={{6,0},{7,1},{8,2},{9,3},{10,4},{11,5},{12,6},{13,7},{14,8},{15,9},... | collective-permute-start | bytes 196616 | tf_op jit(solution)/shard_map/ppermute | solution.py:12
  100.1 1.1 fusion.22
  102.0 1.1 fusion.21
  108.1 1.9 %collective-permute-start.18 = (bf16[256,128]{1,0:T(8,128)(2,1)S(1)}, bf16[256,128]{1,0:T(8,128)(2,1)S(1)}, u32[]{:S(2)}, u32[]{:S(2)}) collective-permute-start(bf16[256,128]{1,0:T(8,128)(2,1)S(1)} %fusion.17), channel_id=1, source_target_pairs={{1,0},{2,1},{3,2},{4,3},{5,4},{6,5},{7,6},{8,7},{9,8},{10,9},{11,1... | collective-permute-start | bytes 196616 | tf_op jit(solution)/shard_map/ppermute | solution.py:12
  110.0 1.9 %collective-permute-start.19 = (bf16[256,128]{1,0:T(8,128)(2,1)}, bf16[256,128]{1,0:T(8,128)(2,1)S(1)}, u32[]{:S(2)}, u32[]{:S(2)}) collective-permute-start(bf16[256,128]{1,0:T(8,128)(2,1)} %fusion.18), channel_id=1, source_target_pairs={{2,0},{3,1},{4,2},{5,3},{6,4},{7,5},{8,6},{9,7},{10,8},{11,9},{12,... | collective-permute-start | bytes 196616 | tf_op jit(solution)/shard_map/ppermute | solution.py:12
  112.0 6.3 %collective-permute-start.20 = (bf16[256,128]{1,0:T(8,128)(2,1)}, bf16[256,128]{1,0:T(8,128)(2,1)S(1)}, u32[]{:S(2)}, u32[]{:S(2)}) collective-permute-start(bf16[256,128]{1,0:T(8,128)(2,1)} %fusion.19), channel_id=1, source_target_pairs={{3,0},{4,1},{5,2},{6,3},{7,4},{8,5},{9,6},{10,7},{11,8},{12,9},{13... | collective-permute-start | bytes 196616 | tf_op jit(solution)/shard_map/ppermute | solution.py:12
  121.9 1.1 fusion.20
  123.0 2.8 %collective-permute-start.21 = (bf16[256,128]{1,0:T(8,128)(2,1)}, bf16[256,128]{1,0:T(8,128)(2,1)}, u32[]{:S(2)}, u32[]{:S(2)}) collective-permute-start(bf16[256,128]{1,0:T(8,128)(2,1)} %fusion.20), channel_id=1, source_target_pairs={{4,0},{5,1},{6,2},{7,3},{8,4},{9,5},{10,6},{11,7},{12,8},{13,9},{1... | collective-permute-start | bytes 196616 | tf_op jit(solution)/shard_map/ppermute | solution.py:12
  125.8 4.3 %collective-permute-start.22 = (bf16[256,128]{1,0:T(8,128)(2,1)}, bf16[256,128]{1,0:T(8,128)(2,1)}, u32[]{:S(2)}, u32[]{:S(2)}) collective-permute-start(bf16[256,128]{1,0:T(8,128)(2,1)} %fusion.21), channel_id=1, source_target_pairs={{5,0},{6,1},{7,2},{8,3},{9,4},{10,5},{11,6},{12,7},{13,8},{14,9},{... | collective-permute-start | bytes 196616 | tf_op jit(solution)/shard_map/ppermute | solution.py:12
  130.1 4.5 %collective-permute-start.23 = (bf16[256,128]{1,0:T(8,128)(2,1)}, bf16[256,128]{1,0:T(8,128)(2,1)}, u32[]{:S(2)}, u32[]{:S(2)}) collective-permute-start(bf16[256,128]{1,0:T(8,128)(2,1)} %fusion.22), channel_id=1, source_target_pairs={{6,0},{7,1},{8,2},{9,3},{10,4},{11,5},{12,6},{13,7},{14,8},{15,9},... | collective-permute-start | bytes 196616 | tf_op jit(solution)/shard_map/ppermute | solution.py:12
  137.2 1.6 %collective-permute-start.28 = (bf16[256,128]{1,0:T(8,128)(2,1)}, bf16[256,128]{1,0:T(8,128)(2,1)S(1)}, u32[]{:S(2)}, u32[]{:S(2)}) collective-permute-start(bf16[256,128]{1,0:T(8,128)(2,1)} %fusion.27), channel_id=1, source_target_pairs={{5,0},{6,1},{7,2},{8,3},{9,4},{10,5},{11,6},{12,7},{13,8},{14,9},{... | collective-permute-start | bytes 196616 | tf_op jit(solution)/shard_map/ppermute | solution.py:12
  138.7 1.9 %collective-permute-start.27 = (bf16[256,128]{1,0:T(8,128)(2,1)}, bf16[256,128]{1,0:T(8,128)(2,1)S(1)}, u32[]{:S(2)}, u32[]{:S(2)}) collective-permute-start(bf16[256,128]{1,0:T(8,128)(2,1)} %fusion.26), channel_id=1, source_target_pairs={{4,0},{5,1},{6,2},{7,3},{8,4},{9,5},{10,6},{11,7},{12,8},{13,9},{1... | collective-permute-start | bytes 196616 | tf_op jit(solution)/shard_map/ppermute | solution.py:12
  140.7 1.9 %collective-permute-start.26 = (bf16[256,128]{1,0:T(8,128)(2,1)}, bf16[256,128]{1,0:T(8,128)(2,1)S(1)}, u32[]{:S(2)}, u32[]{:S(2)}) collective-permute-start(bf16[256,128]{1,0:T(8,128)(2,1)} %fusion.25), channel_id=1, source_target_pairs={{3,0},{4,1},{5,2},{6,3},{7,4},{8,5},{9,6},{10,7},{11,8},{12,9},{13... | collective-permute-start | bytes 196616 | tf_op jit(solution)/shard_map/ppermute | solution.py:12
  142.6 3.1 %collective-permute-start.25 = (bf16[256,128]{1,0:T(8,128)(2,1)}, bf16[256,128]{1,0:T(8,128)(2,1)S(1)}, u32[]{:S(2)}, u32[]{:S(2)}) collective-permute-start(bf16[256,128]{1,0:T(8,128)(2,1)} %fusion.24), channel_id=1, source_target_pairs={{2,0},{3,1},{4,2},{5,3},{6,4},{7,5},{8,6},{9,7},{10,8},{11,9},{12,... | collective-permute-start | bytes 196616 | tf_op jit(solution)/shard_map/ppermute | solution.py:12
  145.7 1.9 %collective-permute-start.24 = (bf16[256,128]{1,0:T(8,128)(2,1)}, bf16[256,128]{1,0:T(8,128)(2,1)S(1)}, u32[]{:S(2)}, u32[]{:S(2)}) collective-permute-start(bf16[256,128]{1,0:T(8,128)(2,1)} %fusion.23), channel_id=1, source_target_pairs={{1,0},{2,1},{3,2},{4,3},{5,4},{6,5},{7,6},{8,7},{9,8},{10,9},{11,1... | collective-permute-start | bytes 196616 | tf_op jit(solution)/shard_map/ppermute | solution.py:12
  147.7 2.0 %convert_add_fusion.1 = f32[256,128]{1,0:T(8,128)} fusion(bf16[256,128]{1,0:T(8,128)(2,1)} %collective-permute-done.23, bf16[256,128]{1,0:T(8,128)(2,1)} %collective-permute-done.22, bf16[256,128]{1,0:T(8,128)(2,1)} %collective-permute-done.21, bf16[256,128]{1,0:T(8,128)(2,1)S(1)} %collective-permute-done.20, ...), kind=kOutput, calls=%fused_computation.105 | convolution fusion | flops 134610944 | bytes 2097152 | tf_op jit(solution)/shard_map/thk,thd->kd/dot_general | solution.py:90
  149.7 2.8 %collective-permute-done.24 = bf16[256,128]{1,0:T(8,128)(2,1)S(1)} collective-permute-done((bf16[256,128]{1,0:T(8,128)(2,1)}, bf16[256,128]{1,0:T(8,128)(2,1)S(1)}, u32[]{:S(2)}, u32[]{:S(2)}) %collective-permute-start.24) | collective-permute-done | bytes 65568 | tf_op jit(solution)/shard_map/ppermute | solution.py:12
  (89 shorter events, 27.1 us)
Async XLA Ops:
  0.6 23.2 %copy-start = (bf16[256,1024]{1,0:T(8,128)(2,1)S(1)}, bf16[256,1024]{1,0:T(8,128)(2,1)}, u32[]{:S(2)}) copy-start(bf16[256,1024]{1,0:T(8,128)(2,1)} %param.5) | copy-start | bytes 1572868
  0.6 12.2 %collective-permute-start.6 = (s32[256]{0:T(256)}, s32[256]{0:T(256)S(1)}, u32[]{:S(2)}, u32[]{:S(2)}) collective-permute-start(s32[256]{0:T(256)} %param.9), channel_id=1, source_target_pairs={{0,4},{1,5},{2,6},{3,7},{4,8},{5,9},{6,10},{7,11},{8,12},{9,13},{1... | collective-permute-start | bytes 3080 | tf_op jit(solution)/shard_map/ppermute | solution.py:12
  3.9 11.7 %collective-permute-start.4 = (s32[256]{0:T(256)}, s32[256]{0:T(256)S(1)}, u32[]{:S(2)}, u32[]{:S(2)}) collective-permute-start(s32[256]{0:T(256)} %param.9), channel_id=1, source_target_pairs={{0,3},{1,4},{2,5},{3,6},{4,7},{5,8},{6,9},{7,10},{8,11},{9,12},{10... | collective-permute-start | bytes 3080 | tf_op jit(solution)/shard_map/ppermute | solution.py:12
  5.9 11.1 %collective-permute-start.2 = (s32[256]{0:T(256)}, s32[256]{0:T(256)S(1)}, u32[]{:S(2)}, u32[]{:S(2)}) collective-permute-start(s32[256]{0:T(256)} %param.9), channel_id=1, source_target_pairs={{0,2},{1,3},{2,4},{3,5},{4,6},{5,7},{6,8},{7,9},{8,10},{9,11},{10,... | collective-permute-start | bytes 3080 | tf_op jit(solution)/shard_map/ppermute | solution.py:12
  7.8 10.4 %collective-permute-start.10 = (s32[256]{0:T(256)}, s32[256]{0:T(256)S(1)}, u32[]{:S(2)}, u32[]{:S(2)}) collective-permute-start(s32[256]{0:T(256)} %param.9), channel_id=1, source_target_pairs={{0,6},{1,7},{2,8},{3,9},{4,10},{5,11},{6,12},{7,13},{8,14},{9,15},... | collective-permute-start | bytes 3080 | tf_op jit(solution)/shard_map/ppermute | solution.py:12
  9.1 11.1 %collective-permute-start.8 = (s32[256]{0:T(256)}, s32[256]{0:T(256)S(1)}, u32[]{:S(2)}, u32[]{:S(2)}) collective-permute-start(s32[256]{0:T(256)} %param.9), channel_id=1, source_target_pairs={{0,5},{1,6},{2,7},{3,8},{4,9},{5,10},{6,11},{7,12},{8,13},{9,14},{... | collective-permute-start | bytes 3080 | tf_op jit(solution)/shard_map/ppermute | solution.py:12
  11.5 13.7 %copy-start.2 = (bf16[256,128]{1,0:T(8,128)(2,1)S(1)}, bf16[256,128]{1,0:T(8,128)(2,1)}, u32[]{:S(2)}) copy-start(bf16[256,128]{1,0:T(8,128)(2,1)} %param.6) | copy-start | bytes 196612
  11.6 15.6 %copy-start.3 = (s32[256]{0:T(256)S(1)}, s32[256]{0:T(256)}, u32[]{:S(2)}) copy-start(s32[256]{0:T(256)} %param.9) | copy-start | bytes 3076
  12.9 12.3 %collective-permute-start = (s32[256]{0:T(256)}, s32[256]{0:T(256)S(1)}, u32[]{:S(2)}, u32[]{:S(2)}) collective-permute-start(s32[256]{0:T(256)} %param.9), channel_id=1, source_target_pairs={{0,1},{1,2},{2,3},{3,4},{4,5},{5,6},{6,7},{7,8},{8,9},{9,10},{10,1... | collective-permute-start | bytes 3080 | tf_op jit(solution)/shard_map/ppermute | solution.py:12
  15.6 81.5 %collective-permute-start.17 = (bf16[256,128]{0,1:T(8,128)(2,1)S(1)}, bf16[256,128]{0,1:T(8,128)(2,1)S(1)}, u32[]{:S(2)}, u32[]{:S(2)}) collective-permute-start(bf16[256,128]{0,1:T(8,128)(2,1)S(1)} %copy.18), channel_id=1, source_target_pairs={{0,6},{1,7},{2,8},{3,9},{4,10},{5,11},{6,12},{7,13},{8,14},{9,15},... | collective-permute-start | bytes 196616 | tf_op jit(solution)/shard_map/ppermute | solution.py:12
  16.9 79.6 %collective-permute-start.16 = (bf16[256,128]{0,1:T(8,128)(2,1)S(1)}, bf16[256,128]{0,1:T(8,128)(2,1)S(1)}, u32[]{:S(2)}, u32[]{:S(2)}) collective-permute-start(bf16[256,128]{0,1:T(8,128)(2,1)S(1)} %copy.18), channel_id=1, source_target_pairs={{0,5},{1,6},{2,7},{3,8},{4,9},{5,10},{6,11},{7,12},{8,13},{9,14},{... | collective-permute-start | bytes 196616 | tf_op jit(solution)/shard_map/ppermute | solution.py:12
  18.2 77.7 %collective-permute-start.15 = (bf16[256,128]{0,1:T(8,128)(2,1)S(1)}, bf16[256,128]{0,1:T(8,128)(2,1)S(1)}, u32[]{:S(2)}, u32[]{:S(2)}) collective-permute-start(bf16[256,128]{0,1:T(8,128)(2,1)S(1)} %copy.18), channel_id=1, source_target_pairs={{0,4},{1,5},{2,6},{3,7},{4,8},{5,9},{6,10},{7,11},{8,12},{9,13},{1... | collective-permute-start | bytes 196616 | tf_op jit(solution)/shard_map/ppermute | solution.py:12
  20.2 67.0 %collective-permute-start.14 = (bf16[256,128]{0,1:T(8,128)(2,1)S(1)}, bf16[256,128]{0,1:T(8,128)(2,1)S(1)}, u32[]{:S(2)}, u32[]{:S(2)}) collective-permute-start(bf16[256,128]{0,1:T(8,128)(2,1)S(1)} %copy.18), channel_id=1, source_target_pairs={{0,3},{1,4},{2,5},{3,6},{4,7},{5,8},{6,9},{7,10},{8,11},{9,12},{10... | collective-permute-start | bytes 196616 | tf_op jit(solution)/shard_map/ppermute | solution.py:12
  25.2 8.1 %collective-permute-start.5 = (bf16[256,128]{1,0:T(8,128)(2,1)S(1)}, bf16[256,128]{1,0:T(8,128)(2,1)S(1)}, u32[]{:S(2)}, u32[]{:S(2)}) collective-permute-start(bf16[256,128]{1,0:T(8,128)(2,1)S(1)} %copy-done.2), channel_id=1, source_target_pairs={{0,3},{1,4},{2,5},{3,6},{4,7},{5,8},{6,9},{7,10},{8,11},{9,12},{10... | collective-permute-start | bytes 196616 | tf_op jit(solution)/shard_map/ppermute | solution.py:12
  33.3 7.4 %collective-permute-start.7 = (bf16[256,128]{1,0:T(8,128)(2,1)S(1)}, bf16[256,128]{1,0:T(8,128)(2,1)S(1)}, u32[]{:S(2)}, u32[]{:S(2)}) collective-permute-start(bf16[256,128]{1,0:T(8,128)(2,1)S(1)} %copy-done.2), channel_id=1, source_target_pairs={{0,4},{1,5},{2,6},{3,7},{4,8},{5,9},{6,10},{7,11},{8,12},{9,13},{1... | collective-permute-start | bytes 196616 | tf_op jit(solution)/shard_map/ppermute | solution.py:12
  40.7 8.1 %collective-permute-start.9 = (bf16[256,128]{1,0:T(8,128)(2,1)S(1)}, bf16[256,128]{1,0:T(8,128)(2,1)S(1)}, u32[]{:S(2)}, u32[]{:S(2)}) collective-permute-start(bf16[256,128]{1,0:T(8,128)(2,1)S(1)} %copy-done.2), channel_id=1, source_target_pairs={{0,5},{1,6},{2,7},{3,8},{4,9},{5,10},{6,11},{7,12},{8,13},{9,14},{... | collective-permute-start | bytes 196616 | tf_op jit(solution)/shard_map/ppermute | solution.py:12
  48.7 7.2 %collective-permute-start.11 = (bf16[256,128]{1,0:T(8,128)(2,1)S(1)}, bf16[256,128]{1,0:T(8,128)(2,1)S(1)}, u32[]{:S(2)}, u32[]{:S(2)}) collective-permute-start(bf16[256,128]{1,0:T(8,128)(2,1)S(1)} %copy-done.2), channel_id=1, source_target_pairs={{0,6},{1,7},{2,8},{3,9},{4,10},{5,11},{6,12},{7,13},{8,14},{9,15},... | collective-permute-start | bytes 196616 | tf_op jit(solution)/shard_map/ppermute | solution.py:12
  56.0 5.0 %collective-permute-start.3 = (bf16[256,128]{1,0:T(8,128)(2,1)S(1)}, bf16[256,128]{1,0:T(8,128)(2,1)S(1)}, u32[]{:S(2)}, u32[]{:S(2)}) collective-permute-start(bf16[256,128]{1,0:T(8,128)(2,1)S(1)} %copy-done.2), channel_id=1, source_target_pairs={{0,2},{1,3},{2,4},{3,5},{4,6},{5,7},{6,8},{7,9},{8,10},{9,11},{10,... | collective-permute-start | bytes 196616 | tf_op jit(solution)/shard_map/ppermute | solution.py:12
  61.0 8.0 %collective-permute-start.1 = (bf16[256,128]{1,0:T(8,128)(2,1)S(1)}, bf16[256,128]{1,0:T(8,128)(2,1)S(1)}, u32[]{:S(2)}, u32[]{:S(2)}) collective-permute-start(bf16[256,128]{1,0:T(8,128)(2,1)S(1)} %copy-done.2), channel_id=1, source_target_pairs={{0,1},{1,2},{2,3},{3,4},{4,5},{5,6},{6,7},{7,8},{8,9},{9,10},{10,1... | collective-permute-start | bytes 196616 | tf_op jit(solution)/shard_map/ppermute | solution.py:12
  68.9 15.1 %collective-permute-start.12 = (bf16[256,128]{0,1:T(8,128)(2,1)S(1)}, bf16[256,128]{0,1:T(8,128)(2,1)S(1)}, u32[]{:S(2)}, u32[]{:S(2)}) collective-permute-start(bf16[256,128]{0,1:T(8,128)(2,1)S(1)} %copy.18), channel_id=1, source_target_pairs={{0,1},{1,2},{2,3},{3,4},{4,5},{5,6},{6,7},{7,8},{8,9},{9,10},{10,1... | collective-permute-start | bytes 196616 | tf_op jit(solution)/shard_map/ppermute | solution.py:12
  81.2 1.1 copy-start.1
  84.0 13.7 %collective-permute-start.13 = (bf16[256,128]{0,1:T(8,128)(2,1)S(1)}, bf16[256,128]{0,1:T(8,128)(2,1)S(1)}, u32[]{:S(2)}, u32[]{:S(2)}) collective-permute-start(bf16[256,128]{0,1:T(8,128)(2,1)S(1)} %copy.18), channel_id=1, source_target_pairs={{0,2},{1,3},{2,4},{3,5},{4,6},{5,7},{6,8},{7,9},{8,10},{9,11},{10,... | collective-permute-start | bytes 196616 | tf_op jit(solution)/shard_map/ppermute | solution.py:12
  87.2 38.5 %collective-permute-start.29 = (bf16[256,128]{1,0:T(8,128)(2,1)S(1)}, bf16[256,128]{1,0:T(8,128)(2,1)S(1)}, u32[]{:S(2)}, u32[]{:S(2)}) collective-permute-start(bf16[256,128]{1,0:T(8,128)(2,1)S(1)} %fusion.28), channel_id=1, source_target_pairs={{6,0},{7,1},{8,2},{9,3},{10,4},{11,5},{12,6},{13,7},{14,8},{15,9},... | collective-permute-start | bytes 196616 | tf_op jit(solution)/shard_map/ppermute | solution.py:12
  108.1 22.0 %collective-permute-start.18 = (bf16[256,128]{1,0:T(8,128)(2,1)S(1)}, bf16[256,128]{1,0:T(8,128)(2,1)S(1)}, u32[]{:S(2)}, u32[]{:S(2)}) collective-permute-start(bf16[256,128]{1,0:T(8,128)(2,1)S(1)} %fusion.17), channel_id=1, source_target_pairs={{1,0},{2,1},{3,2},{4,3},{5,4},{6,5},{7,6},{8,7},{9,8},{10,9},{11,1... | collective-permute-start | bytes 196616 | tf_op jit(solution)/shard_map/ppermute | solution.py:12
  110.0 27.1 %collective-permute-start.19 = (bf16[256,128]{1,0:T(8,128)(2,1)}, bf16[256,128]{1,0:T(8,128)(2,1)S(1)}, u32[]{:S(2)}, u32[]{:S(2)}) collective-permute-start(bf16[256,128]{1,0:T(8,128)(2,1)} %fusion.18), channel_id=1, source_target_pairs={{2,0},{3,1},{4,2},{5,3},{6,4},{7,5},{8,6},{9,7},{10,8},{11,9},{12,... | collective-permute-start | bytes 196616 | tf_op jit(solution)/shard_map/ppermute | solution.py:12
  112.0 26.8 %collective-permute-start.20 = (bf16[256,128]{1,0:T(8,128)(2,1)}, bf16[256,128]{1,0:T(8,128)(2,1)S(1)}, u32[]{:S(2)}, u32[]{:S(2)}) collective-permute-start(bf16[256,128]{1,0:T(8,128)(2,1)} %fusion.19), channel_id=1, source_target_pairs={{3,0},{4,1},{5,2},{6,3},{7,4},{8,5},{9,6},{10,7},{11,8},{12,9},{13... | collective-permute-start | bytes 196616 | tf_op jit(solution)/shard_map/ppermute | solution.py:12
  123.0 17.7 %collective-permute-start.21 = (bf16[256,128]{1,0:T(8,128)(2,1)}, bf16[256,128]{1,0:T(8,128)(2,1)}, u32[]{:S(2)}, u32[]{:S(2)}) collective-permute-start(bf16[256,128]{1,0:T(8,128)(2,1)} %fusion.20), channel_id=1, source_target_pairs={{4,0},{5,1},{6,2},{7,3},{8,4},{9,5},{10,6},{11,7},{12,8},{13,9},{1... | collective-permute-start | bytes 196616 | tf_op jit(solution)/shard_map/ppermute | solution.py:12
  125.8 16.8 %collective-permute-start.22 = (bf16[256,128]{1,0:T(8,128)(2,1)}, bf16[256,128]{1,0:T(8,128)(2,1)}, u32[]{:S(2)}, u32[]{:S(2)}) collective-permute-start(bf16[256,128]{1,0:T(8,128)(2,1)} %fusion.21), channel_id=1, source_target_pairs={{5,0},{6,1},{7,2},{8,3},{9,4},{10,5},{11,6},{12,7},{13,8},{14,9},{... | collective-permute-start | bytes 196616 | tf_op jit(solution)/shard_map/ppermute | solution.py:12
  130.1 15.6 %collective-permute-start.23 = (bf16[256,128]{1,0:T(8,128)(2,1)}, bf16[256,128]{1,0:T(8,128)(2,1)}, u32[]{:S(2)}, u32[]{:S(2)}) collective-permute-start(bf16[256,128]{1,0:T(8,128)(2,1)} %fusion.22), channel_id=1, source_target_pairs={{6,0},{7,1},{8,2},{9,3},{10,4},{11,5},{12,6},{13,7},{14,8},{15,9},... | collective-permute-start | bytes 196616 | tf_op jit(solution)/shard_map/ppermute | solution.py:12
  137.2 12.5 %collective-permute-start.28 = (bf16[256,128]{1,0:T(8,128)(2,1)}, bf16[256,128]{1,0:T(8,128)(2,1)S(1)}, u32[]{:S(2)}, u32[]{:S(2)}) collective-permute-start(bf16[256,128]{1,0:T(8,128)(2,1)} %fusion.27), channel_id=1, source_target_pairs={{5,0},{6,1},{7,2},{8,3},{9,4},{10,5},{11,6},{12,7},{13,8},{14,9},{... | collective-permute-start | bytes 196616 | tf_op jit(solution)/shard_map/ppermute | solution.py:12
  138.7 10.9 %collective-permute-start.27 = (bf16[256,128]{1,0:T(8,128)(2,1)}, bf16[256,128]{1,0:T(8,128)(2,1)S(1)}, u32[]{:S(2)}, u32[]{:S(2)}) collective-permute-start(bf16[256,128]{1,0:T(8,128)(2,1)} %fusion.26), channel_id=1, source_target_pairs={{4,0},{5,1},{6,2},{7,3},{8,4},{9,5},{10,6},{11,7},{12,8},{13,9},{1... | collective-permute-start | bytes 196616 | tf_op jit(solution)/shard_map/ppermute | solution.py:12
  140.7 9.0 %collective-permute-start.26 = (bf16[256,128]{1,0:T(8,128)(2,1)}, bf16[256,128]{1,0:T(8,128)(2,1)S(1)}, u32[]{:S(2)}, u32[]{:S(2)}) collective-permute-start(bf16[256,128]{1,0:T(8,128)(2,1)} %fusion.25), channel_id=1, source_target_pairs={{3,0},{4,1},{5,2},{6,3},{7,4},{8,5},{9,6},{10,7},{11,8},{12,9},{13... | collective-permute-start | bytes 196616 | tf_op jit(solution)/shard_map/ppermute | solution.py:12
  142.6 7.0 %collective-permute-start.25 = (bf16[256,128]{1,0:T(8,128)(2,1)}, bf16[256,128]{1,0:T(8,128)(2,1)S(1)}, u32[]{:S(2)}, u32[]{:S(2)}) collective-permute-start(bf16[256,128]{1,0:T(8,128)(2,1)} %fusion.24), channel_id=1, source_target_pairs={{2,0},{3,1},{4,2},{5,3},{6,4},{7,5},{8,6},{9,7},{10,8},{11,9},{12,... | collective-permute-start | bytes 196616 | tf_op jit(solution)/shard_map/ppermute | solution.py:12
  145.7 6.7 %collective-permute-start.24 = (bf16[256,128]{1,0:T(8,128)(2,1)}, bf16[256,128]{1,0:T(8,128)(2,1)S(1)}, u32[]{:S(2)}, u32[]{:S(2)}) collective-permute-start(bf16[256,128]{1,0:T(8,128)(2,1)} %fusion.23), channel_id=1, source_target_pairs={{1,0},{2,1},{3,2},{4,3},{5,4},{6,5},{7,6},{8,7},{9,8},{10,9},{11,1... | collective-permute-start | bytes 196616 | tf_op jit(solution)/shard_map/ppermute | solution.py:12
where the time goes:
time: 154 us; the launch traced here: 153 us
  starting transfers between devices  82.8 us (54%)
  matrix products  31.3 us (20%)
  waiting for transfers between devices  27.6 us (18%)
  other arithmetic  5.88 us (4%)
  local copies, waits for them, and re-layouts  4.24 us (3%)
    ppermute x30, starting transfers between devices, shifted(): lax.ppermute(value, axis, [(source, source + steps) for source in range(f...  82.8 us
    ppermute x30, waiting for transfers between devices, shifted(): lax.ppermute(value, axis, [(source, source + steps) for source in range(f...  27.6 us
    dot_general x7, matrix products, third_pass(): jnp.einsum('thk,thd->kd', dscore, query_heads, preferred_element_type=jnp...  7.73 us
    dot_general x7, matrix products, third_pass(): jnp.einsum('thk,thd->kd', weight, grad_heads, preferred_element_type=jnp....  6.67 us
    dot_general x7, matrix products, third_pass(): jnp.einsum('thd,kd->thk', grad_heads, entry[1], preferred_element_type=jn...  5.68 us
    unnamed x12, local copies, waits for them, and re-layouts  4.24 us
    dot_general x7, matrix products, second_pass(): jnp.einsum('thk,kd->thd', weight, entry[1], preferred_element_type=jnp.fl...  4.22 us
    dot_general x7, matrix products, scores_of(): jnp.einsum('thd,kd->thk', query_heads, entry_keys, preferred_element_type...  4.2 us
  transfers between devices with their start and end apart: 30, of which 7 were waited for; matrix products, arithmetic and copies ran while one was open for 27% of the time, Pallas kernels for 0%

commit v1 on v0

v1 whole, which is shorter than its diff:
```python
import functools
import math

import jax
import jax.numpy as jnp
from jax import lax
from jax.experimental import pallas as pl
from jax.experimental.pallas import tpu as pltpu
from jax.sharding import PartitionSpec as P

MAXDOC = 1536
AXES = ("seq", "grp")
MESH = pl.DeviceIdType.MESH
F32 = jnp.float32
BF16 = jnp.bfloat16
HIDDEN = -1e30


def dot_nt(a, b):
    return lax.dot_general(a, b, (((1,), (1,)), ((), ())), preferred_element_type=F32)


def dot_nn(a, b):
    return lax.dot_general(a, b, (((1,), (0,)), ((), ())), preferred_element_type=F32)


def kernel(
    groups, total, span,
    q_ref, k_ref, v_ref, g_ref, seg_ref,
    o_ref, dq_ref, dk_ref, dv_ref,
    keys, values, segs, qs, gs, gt, bias, scores, probs, weight,
    row_max, row_sum, row_inv, row_dot,
    gk_out, gv_out, gk_in, gv_in,
    k_send, k_recv, s_send, s_recv, v_send, v_recv, gk_send, gk_recv, gv_send, gv_recv,
):
    tokens, width = k_ref.shape
    heads = q_ref.shape[1] // width
    scale = width ** -0.5
    exponent = scale * math.log2(math.e)
    me = lax.axis_index("seq") * groups + lax.axis_index("grp")

    def device_at(distance):
        where = lax.rem(me + distance + total, total)
        return (lax.div(where, groups), lax.rem(where, groups))

    def rows(d):
        return pl.ds(pl.multiple_of(d * tokens, tokens), tokens)

    def key_copy(d):
        return pltpu.make_async_remote_copy(
            src_ref=k_ref, dst_ref=keys.at[rows(d)], send_sem=k_send.at[d], recv_sem=k_recv.at[d],
            device_id=device_at(d), device_id_type=MESH)

    def seg_copy(d):
        return pltpu.make_async_remote_copy(
            src_ref=seg_ref, dst_ref=segs.at[d], send_sem=s_send.at[d], recv_sem=s_recv.at[d],
            device_id=device_at(d), device_id_type=MESH)

    def value_copy(d):
        return pltpu.make_async_remote_copy(
            src_ref=v_ref, dst_ref=values.at[rows(d)], send_sem=v_send.at[d], recv_sem=v_recv.at[d],
            device_id=device_at(d), device_id_type=MESH)

    def key_grad_copy(d):
        return pltpu.make_async_remote_copy(
            src_ref=gk_out.at[d], dst_ref=gk_in.at[d], send_sem=gk_send.at[d],
            recv_sem=gk_recv.at[d], device_id=device_at(-d), device_id_type=MESH)

    def value_grad_copy(d):
        return pltpu.make_async_remote_copy(
            src_ref=gv_out.at[d], dst_ref=gv_in.at[d], send_sem=gv_send.at[d],
            recv_sem=gv_recv.at[d], device_id=device_at(-d), device_id_type=MESH)

    barrier = pltpu.get_barrier_semaphore()
    for d in range(1, span + 1):
        for way in (d, -d):
            pl.semaphore_signal(barrier, inc=1, device_id=device_at(way), device_id_type=MESH)

    keys[pl.ds(0, tokens), :] = k_ref[...]
    values[pl.ds(0, tokens), :] = v_ref[...]
    segs[0] = seg_ref[...]
    for h in range(heads):
        stacked = pl.ds(h * tokens, tokens)
        head = pl.ds(h * width, width)
        qs[stacked, :] = q_ref[:, head]
        gs[stacked, :] = g_ref[:, head]
        gt[:, stacked] = g_ref[:, head].T
    row_max[...] = jnp.full(row_max.shape, HIDDEN, F32)
    row_sum[...] = jnp.zeros(row_sum.shape, F32)

    pl.semaphore_wait(barrier, 2 * span)
    for d in range(1, span + 1):
        key_copy(d).start()
        seg_copy(d).start()
    for d in range(1, span + 1):
        value_copy(d).start()

    def score_pass(d, carry):
        @pl.when(d > 0)
        def _():
            key_copy(d).wait_recv()
            seg_copy(d).wait_recv()

        key_block = keys[rows(d), :]
        seg_column = jnp.broadcast_to(segs[d][0:1, :], (128, tokens)).T
        seg_key = jnp.concatenate([seg_column] * (tokens // 128), axis=1)
        key_at = lax.broadcasted_iota(jnp.int32, (tokens, tokens), 0) - d * tokens
        query_at = lax.broadcasted_iota(jnp.int32, (tokens, tokens), 1)
        first = jnp.where(me >= d, -d * tokens, tokens)
        visible = (seg_key == seg_ref[0:1, :]) & (key_at <= query_at) & (key_at >= first)
        bias[...] = jnp.where(visible, 0.0, HIDDEN)
        for h in range(heads):
            cols = pl.ds(h * tokens, tokens)
            score = dot_nt(key_block, qs[cols, :]) + bias[...]
            scores[rows(d), cols] = score
            top = jnp.max(score.reshape(tokens // 8, 8, tokens), axis=0)
            row_max[:, cols] = jnp.maximum(row_max[:, cols], top)
        return carry

    lax.fori_loop(0, span + 1, score_pass, 0)
    row_max[...] = jnp.broadcast_to(jnp.max(row_max[...], axis=0, keepdims=True), row_max.shape)

    def exp_pass(d, carry):
        for h in range(heads):
            cols = pl.ds(h * tokens, tokens)
            part = jnp.exp2((scores[rows(d), cols] - row_max[0:1, cols]) * exponent)
            row_sum[:, cols] += jnp.sum(part.reshape(tokens // 8, 8, tokens), axis=0)
            probs[rows(d), cols] = part.astype(BF16)
        return carry

    lax.fori_loop(0, span + 1, exp_pass, 0)
    for d in range(1, span + 1):
        value_copy(d).wait_recv()
    values_t = values[...].T
    for h in range(heads):
        cols = pl.ds(h * tokens, tokens)
        inverse = 1.0 / jnp.sum(row_sum[:, cols], axis=0, keepdims=True)
        attended = (dot_nn(values_t, probs[:, cols]) * inverse).astype(BF16)
        dot = jnp.sum(attended.astype(F32) * gt[:, cols].astype(F32), axis=0, keepdims=True)
        row_inv[:, cols] = jnp.broadcast_to(inverse, (8, tokens))
        row_dot[:, cols] = jnp.broadcast_to(dot, (8, tokens))
        o_ref[:, pl.ds(h * width, width)] = attended.T

    def grad_pass(step, carry):
        d = span - step
        value_block = values[rows(d), :]
        for h in range(heads):
            cols = pl.ds(h * tokens, tokens)
            dprob = dot_nt(value_block, gs[cols, :])
            prob = probs[rows(d), cols].astype(F32) * row_inv[0:1, cols]
            weight[:, cols] = prob.astype(BF16)
            probs[rows(d), cols] = (prob * (dprob - row_dot[0:1, cols])).astype(BF16)
        key_part = dot_nn(probs[rows(d), :], qs[...]) * scale
        value_part = dot_nn(weight[...], gs[...])

        @pl.when(d > 0)
        def _():
            gk_out[d] = key_part.astype(BF16)
            gv_out[d] = value_part.astype(BF16)
            key_grad_copy(d).start()
            value_grad_copy(d).start()

        @pl.when(d == 0)
        def _():
            dk_ref[...] = key_part
            dv_ref[...] = value_part

        return carry

    lax.fori_loop(0, span + 1, grad_pass, 0)
    keys_t = keys[...].T
    for h in range(heads):
        cols = pl.ds(h * tokens, tokens)
        grad = (dot_nn(keys_t, probs[:, cols]) * scale).astype(BF16)
        dq_ref[:, pl.ds(h * width, width)] = grad.T
    for d in range(span, 0, -1):
        key_grad_copy(d).wait_recv()
        value_grad_copy(d).wait_recv()
        dk_ref[...] += gk_in[d].astype(F32)
        dv_ref[...] += gv_in[d].astype(F32)
    for d in range(1, span + 1):
        key_copy(d).wait_send()
        seg_copy(d).wait_send()
        value_copy(d).wait_send()
        key_grad_copy(d).wait_send()
        value_grad_copy(d).wait_send()


def on_device(queries, key_rows, value_rows, out_grad, segment):
    tokens, width = key_rows.shape
    heads = queries.shape[1] // width
    groups = lax.axis_size("grp")
    total = groups * lax.axis_size("seq")
    span = -(-MAXDOC // tokens)
    blocks = span + 1
    stacked = heads * tokens
    seg_rows = jnp.broadcast_to(segment.astype(F32)[None, :], (8, tokens))
    vmem = pl.BlockSpec(memory_space=pltpu.VMEM)
    sems = pltpu.SemaphoreType.DMA((blocks,))
    return pl.pallas_call(
        functools.partial(kernel, groups, total, span),
        out_shape=(
            jax.ShapeDtypeStruct(queries.shape, BF16),
            jax.ShapeDtypeStruct(queries.shape, BF16),
            jax.ShapeDtypeStruct(key_rows.shape, F32),
            jax.ShapeDtypeStruct(key_rows.shape, F32),
        ),
        in_specs=[vmem] * 5,
        out_specs=(vmem,) * 4,
        scratch_shapes=[
            pltpu.VMEM((blocks * tokens, width), BF16),
            pltpu.VMEM((blocks * tokens, width), BF16),
            pltpu.VMEM((blocks, 8, tokens), F32),
            pltpu.VMEM((stacked, width), BF16),
            pltpu.VMEM((stacked, width), BF16),
            pltpu.VMEM((width, stacked), BF16),
            pltpu.VMEM((tokens, tokens), F32),
            pltpu.VMEM((blocks * tokens, stacked), F32),
            pltpu.VMEM((blocks * tokens, stacked), BF16),
            pltpu.VMEM((tokens, stacked), BF16),
            pltpu.VMEM((8, stacked), F32),
            pltpu.VMEM((8, stacked), F32),
            pltpu.VMEM((8, stacked), F32),
            pltpu.VMEM((8, stacked), F32),
            pltpu.VMEM((blocks, tokens, width), BF16),
            pltpu.VMEM((blocks, tokens, width), BF16),
            pltpu.VMEM((blocks, tokens, width), BF16),
            pltpu.VMEM((blocks, tokens, width), BF16),
        ]
        + [sems] * 10,
        compiler_params=pltpu.CompilerParams(
            collective_id=0, has_side_effects=True, vmem_limit_bytes=60 * 1024 * 1024
        ),
    )(queries, key_rows, value_rows, out_grad, seg_rows)


def solution(mesh):
    in_specs = (P(AXES, None), P(AXES, None), P(AXES, None), P(AXES, None), P(AXES))
    out_specs = (P(AXES, None),) * 4
    return jax.shard_map(
        on_device, mesh=mesh, in_specs=in_specs, out_specs=out_specs, check_vma=False
    )
```

time: 154 us -> 51.5 us (0.33)
  the two profiles are of different devices: /device:TPU:27 before, /device:TPU:0 now
where the time goes in v1:
time: 51.5 us; the launch traced here: 51.3 us
  Pallas kernels  44.8 us (87%)
  local copies, waits for them, and re-layouts  5.16 us (10%)
  other arithmetic  0.68 us (1%)
  between operations  0.65 us (1%)
    pallas_call x1, Pallas kernels, on_device(): pl.pallas_call(functools.partial(kernel, groups, total, span), out_shape=...  44.8 us
    unnamed x10, local copies, waits for them, and re-layouts  4.56 us

profile of v1, /device:TPU:0, one launch (start us, length us, event | category | flops | bytes accessed | tf_op | source)
XLA Modules:
  0.0 51.3 jit_solution(15595019477881107642)
XLA Ops:
  0.6 0.7 %convert_element_type.3 = f32[256]{0:T(256)S(1)} convert(s32[256]{0:T(256)} %param.9) | non-fusion elementwise | flops 256 | bytes 2048 | tf_op jit(solution)/shard_map/convert_element_type | solution.py:197
  1.3 0.6 %broadcast_in_dim.2.seg_ref = f32[8,256]{1,0:T(8,128)} broadcast(f32[256]{0:T(256)S(1)} %convert_element_type.3), dimensions={1} | broadcast | bytes 9216 | tf_op jit(solution)/shard_map/broadcast_in_dim | solution.py:197
  1.9 44.8 %shard_map.84 = (bf16[256,1024]{1,0:T(8,128)(2,1)}, bf16[256,1024]{1,0:T(8,128)(2,1)}, f32[256,128]{1,0:T(8,128)}, f32[256,128]{1,0:T(8,128)}) custom-call(bf16[256,1024]{1,0:T(8,128)(2,1)} %q_ref.1, bf16[256,128]{1,0:T(8,128)(2,1)} %k_ref.1, bf16[256,128]{1,0:T(8,128)(2,1)} %v_ref.1, bf16[256,1024]{1,0:T(8,128)(2,1)} %g_ref.1, f32[8,256]{1,0:T(8,128)} %broadcast_in_dim.2.seg_ref), custom_call_target="tpu_custom_call" | custom-call | tf_op jit(solution)/shard_map/pallas_call | solution.py:200
  46.8 0.0 copy-start
  46.8 1.9 %copy.13 = bf16[256,1024]{1,0:T(8,128)(2,1)} copy(bf16[256,1024]{1,0:T(8,128)(2,1)} %get-tuple-element.8) | data formatting | bytes 1048576
  48.7 0.0 copy-done
  48.7 0.0 copy-start.2
  48.7 0.8 %copy.14 = bf16[256,1024]{1,0:T(8,128)(2,1)} copy(bf16[256,1024]{1,0:T(8,128)(2,1)S(1)} %copy-done) | data formatting | bytes 1048576
  49.5 0.2 copy-done.2
  49.7 0.0 copy-start.1
  49.7 0.7 %copy.15 = f32[256,128]{1,0:T(8,128)} copy(f32[256,128]{1,0:T(8,128)S(1)} %copy-done.2) | data formatting | bytes 262144
  50.4 0.3 copy-done.1
  50.7 0.7 %copy.16 = f32[256,128]{1,0:T(8,128)} copy(f32[256,128]{1,0:T(8,128)S(1)} %copy-done.1) | data formatting | bytes 262144
Async XLA Ops:
  46.8 1.9 %copy-start = (bf16[256,1024]{1,0:T(8,128)(2,1)S(1)}, bf16[256,1024]{1,0:T(8,128)(2,1)}, u32[]{:S(2)}) copy-start(bf16[256,1024]{1,0:T(8,128)(2,1)} %get-tuple-element.9) | copy-start | bytes 1572868
  48.7 1.0 %copy-start.2 = (f32[256,128]{1,0:T(8,128)S(1)}, f32[256,128]{1,0:T(8,128)}, u32[]{:S(2)}) copy-start(f32[256,128]{1,0:T(8,128)} %get-tuple-element.10) | copy-start | bytes 393220
  49.7 1.0 %copy-start.1 = (f32[256,128]{1,0:T(8,128)S(1)}, f32[256,128]{1,0:T(8,128)}, u32[]{:S(2)}) copy-start(f32[256,128]{1,0:T(8,128)} %get-tuple-element.11) | copy-start | bytes 393220
